TPU v7x, 512 devices: a whole 4x8x8 slice. The times are simulated.
512 devices in a mesh: year: 32 (over x_hi, y, core), port: 16 (over z, x_lo).
Axes of the slice: x: 4 (x_hi: 2, x_lo: 2; x = x_hi * 2 + x_lo), y: 8, z: 8, core: 2. Of those that a mesh axis runs over, the one named last changes fastest.
Arguments:
- event_loss: bfloat16 [16384, 16384], P('year', 'port'), may hold values from 0 to 24
- event_year: int32 [16384], P('year'), may hold values from -1 to 1023, as said below
- retention: float32 [16384], P('port'), may hold values from 0.2 to 2
- risk_limit: float32 [16384], P('port'), may hold values from 1 to 8
- cession_share: bfloat16 [16384, 4], P('port'), may hold values from 0.099609375 to 1
- member_treaty: int32 [16384, 4], P('port'), may hold values from 0 to 1023, all different within a row
- attach_tier: int32 [1024], P('port'), may hold values from 2 to 11
- limit_tier: int32 [1024], P('port'), may hold values from 2 to 10
- reinstatements: int32 [1024], P('port'), may hold values from 0 to 3
- reinstate_rate: float32 [1024], P('port'), may hold values from 0.1 to 1
- stop_attach: float32 [1024], P('port'), may hold values from 0.7 to 2
- stop_width: float32 [1024], P('port'), may hold values from 0.3 to 2
Outputs:
- layer_net: float32 [1024, 1024], P('port', 'year')
- stop_loss: float32 [1024, 1024], P('port', 'year')
- tail_mean: float32 [1024], P('port')
Inputs may be any that keep to these rules, and one draw needn't show every extreme that they name: `event_year`: the 512 rows of year-block b name years b * 32 to (b + 1) * 32 - 1 in nondecreasing order, followed by padding rows marked -1; at least one block has no padding row. `member_treaty`: each portfolio names 4 different treaties, and every treaty is named by some portfolio.
All inputs are finite; a program needn't handle non-finite values.
Results may differ from a plain program's by a relative error of at most 0.029.
Values may be sent and summed in bfloat16 or wider, within the bound.
No kernel may reach another device: no remote copies, remote signals or barrier semaphores. Data moves between devices by JAX's collectives and lax.ppermute only.
A program may use at most 64 MiB of HBM per device.

v0:
```python
import jax
import jax.numpy as jnp
from jax import lax
from jax.sharding import PartitionSpec as P

TREATIES = 1024
MEMB = 4
YEAR_DEV = 32
TAIL = 16


UNIT_LOSS = 1.0


def in_blocks(x, dim, count):
    before, after = (x.shape[:dim], x.shape[dim + 1 :])
    return jnp.moveaxis(x.reshape(*before, count, -1, *after), dim, 0)


def sum_at_owner(x, axis, dim):
    count = lax.axis_size(axis)
    blocks = lax.all_to_all(in_blocks(x, dim, count), axis, 0, 0, tiled=True)
    return jnp.sum(blocks.astype(jnp.float32), axis=0)


def from_everyone(x, axis):
    count = lax.axis_size(axis)
    return lax.all_to_all(jnp.broadcast_to(x[None], (count, *x.shape)), axis, 0, 0, tiled=True)


def gathered_once(x, axis):
    leaves = jax.tree.leaves(x)
    turns = sorted(range(len(leaves)), key=lambda k: -leaves[k].size)
    width = (1, *leaves[turns[0]].shape)[-1]
    lines = [
        jnp.pad(leaves[k].reshape(-1), (0, -leaves[k].size % width)).reshape(-1, width)
        for k in turns
    ]
    both, at, found = (from_everyone(jnp.concatenate(lines), axis), 0, {})
    for k, line in zip(turns, lines):
        section = both[:, at : at + len(line)].reshape(len(both), -1)
        found[k] = section[:, : leaves[k].size].reshape(-1, *leaves[k].shape)
        at += len(line)
    numbers = iter(range(len(leaves)))
    return jax.tree.map(lambda _: found[next(numbers)], x)


def combined_pairwise(pieces, combine):
    while len(jax.tree.leaves(pieces)[0]) > 1:
        pieces = jax.vmap(combine)(
            *(jax.tree.map(lambda part: part[side::2], pieces) for side in (0, 1))
        )
    return jax.tree.map(lambda part: part[0], pieces)


def combined_all(x, axis, combine):
    pieces = gathered_once(x, axis)
    return combined_pairwise(pieces, combine)


def clamp_between(values, lower, upper):
    return jnp.minimum(jnp.maximum(values, lower), upper)


def top_years(values, keep_count):
    return jnp.sort(values, axis=1)[:, values.shape[1] - keep_count :]


def on_device(
    event_loss,
    event_year,
    retention,
    risk_limit,
    cession_share,
    member_treaty,
    attach_tier,
    limit_tier,
    reinstatements,
    reinstate_rate,
    stop_attach,
    stop_width,
):
    own_count = attach_tier.shape[0]
    ceded_loss = clamp_between(
        event_loss.astype(jnp.float32) - retention[None, :], 0.0, risk_limit[None, :]
    ).astype(jnp.bfloat16)
    treaty_ids = lax.broadcasted_iota(jnp.int32, (1, TREATIES), 1)
    weights = jnp.zeros((event_loss.shape[1], TREATIES), jnp.float32)
    for member_slot in range(MEMB):
        picked = member_treaty[:, member_slot : member_slot + 1] == treaty_ids
        weights = weights + jnp.where(
            picked, cession_share[:, member_slot : member_slot + 1].astype(jnp.float32), 0.0
        )
    weights = weights.astype(jnp.bfloat16)
    first_year = lax.axis_index("year") * YEAR_DEV
    local_year = event_year - first_year
    contract = (((0,), (1,)), ((), ()))
    event_treaty = sum_at_owner(
        lax.dot_general(weights, ceded_loss, contract, preferred_element_type=jnp.float32).astype(
            jnp.bfloat16
        ),
        "port",
        0,
    )
    attach = attach_tier.astype(jnp.float32) * UNIT_LOSS
    limit_loss = limit_tier.astype(jnp.float32) * UNIT_LOSS
    recovered = clamp_between(event_treaty - attach[:, None], 0.0, limit_loss[:, None])
    retained = event_treaty - recovered
    year_hits = (local_year[:, None] == lax.broadcasted_iota(jnp.int32, (1, YEAR_DEV), 1)).astype(
        jnp.float32
    )
    yearly = jnp.dot(
        jnp.concatenate((recovered, retained), 0), year_hits, preferred_element_type=jnp.float32
    )
    annual = yearly[:own_count]
    kept_annual = yearly[own_count:]
    reinstated = reinstatements.astype(jnp.float32)
    layer_paid = jnp.minimum(annual, ((1.0 + reinstated) * limit_loss)[:, None])
    layer_net = (
        layer_paid
        - reinstate_rate[:, None] * jnp.minimum(layer_paid, (reinstated * limit_loss)[:, None])
    ) / limit_loss[:, None]
    year_total = YEAR_DEV * lax.axis_size("year")

    def join_stats(earlier, later):
        return (earlier[0] + later[0], top_years(jnp.concatenate((earlier[1], later[1]), 1), TAIL))

    summed, largest = combined_all(
        (jnp.sum(kept_annual, axis=1), top_years(kept_annual, TAIL)), "year", join_stats
    )
    base_loss = UNIT_LOSS + summed / year_total
    loss_ratio = kept_annual / base_loss[:, None]
    tail_mean = jnp.mean(largest / base_loss[:, None], axis=1)
    stop_loss = clamp_between(loss_ratio - stop_attach[:, None], 0.0, stop_width[:, None])
    return (layer_net, stop_loss, tail_mean)


def solution(mesh):
    return jax.shard_map(
        on_device,
        mesh=mesh,
        in_specs=(
            P("year", "port"),
            P("year"),
            P("port"),
            P("port"),
            P("port", None),
            P("port", None),
            P("port"),
            P("port"),
            P("port"),
            P("port"),
            P("port"),
            P("port"),
        ),
        out_specs=(P("port", "year"), P("port", "year"), P("port")),
        check_vma=False,
    )
```

profile of v0, /device:TPU:1, one launch (start us, length us, event | category | flops | bytes accessed | tf_op | source)
XLA Modules:
  0.0 93.5 jit_solution(6935008694154809549)
XLA Ops:
  0.6 0.9 fusion.32
  1.5 0.9 slice_convert_fusion.3
  2.4 5.5 %fusion.10 = bf16[1024,512]{1,0:T(8,128)(2,1)} fusion(f32[1024]{0:T(1024)S(1)} %bitcast.24, s32[1024]{0:T(1024)S(1)} %bitcast.20, f32[1024]{0:T(1024)S(1)} %bitcast.25, s32[1024]{0:T(1024)S(1)} %bitcast.21, f32[1024]{0:T(1024)S(1)} %bitcast.23, s32[1024]{0:T(1024)S(1)} %bitcast.19, f32[1024]{0:T(1024)S(1)} %bitcast.22, s32[1024]{0:T(1024)S(1)} %bitcast.18, ...), kind=kOutput, calls=%fused_computation.17 | convolution fusion | flops 1089994752 | bytes 2138112 | tf_op jit(solution)/shard_map/dot_general | solution.py:99
  7.8 12.0 %all-to-all-start = ((bf16[16,64,512]{2,1,0:T(8,128)(2,1)}), bf16[16,64,512]{2,1,0:T(8,128)(2,1)S(1)}, u32[]{:S(2)}, u32[]{:S(2)}) async-start(bf16[16,64,512]{2,1,0:T(8,128)(2,1)} %bitcast.8), calls=%async_computation | async-start | bytes 2097152 | tf_op jit(solution)/shard_map/all_to_all | solution.py:22
  19.9 25.3 %all-to-all-done = bf16[16,64,512]{2,1,0:T(8,128)(2,1)S(1)} async-done(((bf16[16,64,512]{2,1,0:T(8,128)(2,1)}), bf16[16,64,512]{2,1,0:T(8,128)(2,1)S(1)}, u32[]{:S(2)}, u32[]{:S(2)}) %all-to-all-start) | async-done | bytes 1048608 | tf_op jit(solution)/shard_map/all_to_all | solution.py:22
  45.3 0.1 convert_reduce_fusion
  45.5 0.3 fusion.14
  46.0 0.9 sort.90
  47.1 0.7 broadcast_in_dim.82
  47.8 13.7 %all-to-all-start.1 = ((f32[32,68,16]{1,2,0:T(8,128)}), f32[32,68,16]{1,2,0:T(8,128)S(1)}, u32[]{:S(2)}, u32[]{:S(2)}) async-start(f32[32,68,16]{1,2,0:T(8,128)} %broadcast_in_dim.82), calls=%async_computation.1 | async-start | bytes 524288 | tf_op jit(solution)/shard_map/all_to_all | solution.py:28
  61.5 13.0 %all-to-all-done.1 = f32[32,68,16]{1,2,0:T(8,128)S(1)} async-done(((f32[32,68,16]{1,2,0:T(8,128)}), f32[32,68,16]{1,2,0:T(8,128)S(1)}, u32[]{:S(2)}, u32[]{:S(2)}) %all-to-all-start.1) | async-done | bytes 139296 | tf_op jit(solution)/shard_map/all_to_all | solution.py:28
  74.7 0.2 copy.18
  74.9 0.2 slice.130
  75.1 0.2 slice.131
  75.3 0.1 slice.132
  75.5 0.1 slice.133
  76.1 7.5 %sort.91 = (f32[16,64,32]{1,2,0:T(8,128)S(1)}, s32[16,64,32]{1,2,0:T(8,128)}) sort(f32[16,64,32]{1,2,0:T(8,128)S(1)} %pad_maximum_fusion, s32[16,64,32]{1,2,0:T(8,128)S(1)} %iota.29), dimensions={2}, to_apply=%region_3.4 | sort | flops 491520 | bytes 524288 | tf_op jit(solution)/shard_map/vmap(jit(sort))/sort | solution.py:66
  83.7 3.9 %sort.92 = (f32[8,64,32]{1,2,0:T(8,128)S(1)}, s32[8,64,32]{1,2,0:T(8,128)}) sort(f32[8,64,32]{1,2,0:T(8,128)S(1)} %pad_maximum_fusion.1, s32[8,64,32]{1,2,0:T(8,128)S(1)} %iota.30), dimensions={2}, to_apply=%region_4.5 | sort | flops 229376 | bytes 262144 | tf_op jit(solution)/shard_map/vmap(jit(sort))/sort | solution.py:66
  87.7 2.1 %sort.93 = (f32[4,64,32]{1,2,0:T(8,128)S(1)}, s32[4,64,32]{1,2,0:T(8,128)}) sort(f32[4,64,32]{1,2,0:T(8,128)S(1)} %pad_maximum_fusion.2, s32[4,64,32]{1,2,0:T(8,128)S(1)} %iota.31), dimensions={2}, to_apply=%region_5.6 | sort | flops 106496 | bytes 131072 | tf_op jit(solution)/shard_map/vmap(jit(sort))/sort | solution.py:66
  89.9 1.2 %sort.94 = (f32[2,64,32]{1,2,0:T(8,128)S(1)}, s32[2,64,32]{1,2,0:T(8,128)}) sort(f32[2,64,32]{1,2,0:T(8,128)S(1)} %pad_maximum_fusion.3, s32[2,64,32]{1,2,0:T(8,128)S(1)} %iota.32), dimensions={2}, to_apply=%region_6.7 | sort | flops 49152 | bytes 65536 | tf_op jit(solution)/shard_map/vmap(jit(sort))/sort | solution.py:66
  91.2 0.2 fusion.21
  91.4 0.9 sort.95
  92.3 0.5 broadcast_multiply_fusion
  92.8 0.7 maximum_minimum_fusion.1
  (53 shorter events, 1.2 us)
Async XLA Ops:
  7.8 12.0 %copy-start.4 = (s32[64]{0:T(128)S(1)}, s32[64]{0:T(128)}, u32[]{:S(2)}) copy-start(s32[64]{0:T(128)} %param.19) | copy-start | bytes 772
  7.8 12.1 %copy-start.6 = (s32[64]{0:T(128)S(1)}, s32[64]{0:T(128)}, u32[]{:S(2)}) copy-start(s32[64]{0:T(128)} %param.18) | copy-start | bytes 772
  7.8 12.1 %copy-start = (s32[512]{0:T(512)S(1)}, s32[512]{0:T(512)}, u32[]{:S(2)}) copy-start(s32[512]{0:T(512)} %param.13) | copy-start | bytes 6148
  7.8 37.4 %all-to-all-start = ((bf16[16,64,512]{2,1,0:T(8,128)(2,1)}), bf16[16,64,512]{2,1,0:T(8,128)(2,1)S(1)}, u32[]{:S(2)}, u32[]{:S(2)}) async-start(bf16[16,64,512]{2,1,0:T(8,128)(2,1)} %bitcast.8), calls=%async_computation | async-start | bytes 2097152 | tf_op jit(solution)/shard_map/all_to_all | solution.py:22
  19.9 41.6 %copy-start.5 = (s32[64]{0:T(128)S(1)}, s32[64]{0:T(128)}, u32[]{:S(2)}) copy-start(s32[64]{0:T(128)} %param.20) | copy-start | bytes 772
  47.8 26.7 %all-to-all-start.1 = ((f32[32,68,16]{1,2,0:T(8,128)}), f32[32,68,16]{1,2,0:T(8,128)S(1)}, u32[]{:S(2)}, u32[]{:S(2)}) async-start(f32[32,68,16]{1,2,0:T(8,128)} %broadcast_in_dim.82), calls=%async_computation.1 | async-start | bytes 524288 | tf_op jit(solution)/shard_map/all_to_all | solution.py:28
  83.7 9.2 %copy-start.1 = (f32[64]{0:T(128)S(1)}, f32[64]{0:T(128)}, u32[]{:S(2)}) copy-start(f32[64]{0:T(128)} %param.23) | copy-start | bytes 772
  83.7 9.1 %copy-start.2 = (f32[64]{0:T(128)S(1)}, f32[64]{0:T(128)}, u32[]{:S(2)}) copy-start(f32[64]{0:T(128)} %param.22) | copy-start | bytes 772
  83.7 9.1 %copy-start.3 = (f32[64]{0:T(128)S(1)}, f32[64]{0:T(128)}, u32[]{:S(2)}) copy-start(f32[64]{0:T(128)} %param.21) | copy-start | bytes 772
where the time goes:
time: 93.9 us; the launch traced here: 93.5 us
  waiting for transfers between devices  38.4 us (41%)
  starting transfers between devices  25.7 us (27%)
  other arithmetic  19.5 us (21%)
  matrix products  5.73 us (6%)
  local copies, waits for them, and re-layouts  3.25 us (3%)
  between operations  0.97 us (1%)
    all_to_all x1, waiting for transfers between devices, sum_at_owner(): blocks = lax.all_to_all(in_blocks(x, dim, count), axis, 0, 0, tiled=True)  25.3 us
    sort x6, other arithmetic, top_years(): return jnp.sort(values, axis=1)[:, values.shape[1] - keep_count:]  16.7 us
    all_to_all x1, starting transfers between devices, from_everyone(): lax.all_to_all(jnp.broadcast_to(x[None], (count, *x.shape)), axis, 0, 0,...  13.7 us
    all_to_all x1, waiting for transfers between devices, from_everyone(): lax.all_to_all(jnp.broadcast_to(x[None], (count, *x.shape)), axis, 0, 0,...  13 us
    all_to_all x1, starting transfers between devices, sum_at_owner(): blocks = lax.all_to_all(in_blocks(x, dim, count), axis, 0, 0, tiled=True)  12 us
    dot_general x1, matrix products, on_device(): lax.dot_general(weights, ceded_loss, contract, preferred_element_type=jnp...  5.45 us
  transfers between devices with their start and end apart: 2, of which 2 were waited for; matrix products, arithmetic and copies ran while one was open for 0% of the time, Pallas kernels for 0%

commit v1 on v0

v1 whole, which is shorter than its diff:
```python
import jax
import jax.numpy as jnp
from jax import lax
from jax.experimental import pallas as pl
from jax.experimental.pallas import tpu as pltpu
from jax.sharding import PartitionSpec as P

TREATIES = 1024
MEMB = 4
YEAR_DEV = 32
TAIL = 16
LANES = 128
BLOCK = 256

UNIT_LOSS = 1.0

VMEM = pl.BlockSpec(memory_space=pltpu.VMEM)
ANY = pl.BlockSpec(memory_space=pl.ANY)
PARAMS = pltpu.CompilerParams(vmem_limit_bytes=16 * 1024 * 1024)
BY_ROWS = (((1,), (1,)), ((), ()))


def clamp_between(values, lower, upper):
    return jnp.minimum(jnp.maximum(values, lower), upper)


def shard_sums_kernel(
    loss_hbm, retention, risk_limit, share, member, sums, loss, weights, ceded, arrived
):
    fetch = pltpu.make_async_copy(loss_hbm, loss, arrived)
    fetch.start()
    columns = loss.shape[1]
    treaty = lax.broadcasted_iota(jnp.int32, (BLOCK, LANES), 0)
    treaty = treaty.astype(jnp.float32).astype(jnp.bfloat16)
    zero = jnp.zeros((BLOCK, LANES), jnp.bfloat16)
    named = member[...]
    part = share[...]
    for first in range(0, TREATIES, BLOCK):
        local = named - first
        inside = (local >= 0) & (local < BLOCK)
        local = jnp.where(inside, local, BLOCK).astype(jnp.float32).astype(jnp.bfloat16)
        for at in range(0, columns, LANES):
            block = zero
            for slot in range(MEMB):
                hit = treaty == local[slot : slot + 1, at : at + LANES]
                block = jnp.where(hit, part[slot : slot + 1, at : at + LANES], block)
            weights[first : first + BLOCK, at : at + LANES] = block
    fetch.wait()
    ceded[...] = clamp_between(
        loss[...].astype(jnp.float32) - retention[...], 0.0, risk_limit[...]
    ).astype(jnp.bfloat16)
    for first in range(0, TREATIES, BLOCK):
        sums[first : first + BLOCK, :] = lax.dot_general(
            weights[first : first + BLOCK, :],
            ceded[...],
            BY_ROWS,
            preferred_element_type=jnp.float32,
        ).astype(jnp.bfloat16)


def shard_sums(event_loss, retention, risk_limit, cession_share, member_treaty):
    rows, columns = event_loss.shape
    return pl.pallas_call(
        shard_sums_kernel,
        out_shape=jax.ShapeDtypeStruct((TREATIES, rows), jnp.bfloat16),
        in_specs=[ANY, VMEM, VMEM, VMEM, VMEM],
        out_specs=VMEM,
        scratch_shapes=[
            pltpu.VMEM((rows, columns), jnp.bfloat16),
            pltpu.VMEM((TREATIES, columns), jnp.bfloat16),
            pltpu.VMEM((rows, columns), jnp.bfloat16),
            pltpu.SemaphoreType.DMA,
        ],
        compiler_params=PARAMS,
        name="shard_sums",
    )(
        event_loss,
        retention.reshape(1, -1),
        risk_limit.reshape(1, -1),
        cession_share.T,
        member_treaty.T,
    )


def as_column(row):
    count = row.shape[1]
    down = lax.broadcasted_iota(jnp.int32, (count, count), 0)
    across = lax.broadcasted_iota(jnp.int32, (count, count), 1)
    return jnp.sum(jnp.where(down == across, row, 0.0), axis=1, keepdims=True)


def in_two(values):
    high = values.astype(jnp.bfloat16)
    low = (values - high.astype(jnp.float32)).astype(jnp.bfloat16)
    return [high, low]


def annual_kernel(
    blocks, event_year, attach_tier, limit_tier, reinstatements, reinstate_rate, net, kept, sent
):
    count = attach_tier.shape[1]
    total = blocks[0].astype(jnp.float32)
    for shard in range(1, blocks.shape[0]):
        total = total + blocks[shard].astype(jnp.float32)
    attach = attach_tier[...].astype(jnp.float32) * UNIT_LOSS
    limit = limit_tier[...].astype(jnp.float32) * UNIT_LOSS
    recovered = clamp_between(total - as_column(attach), 0.0, as_column(limit))
    retained = total - recovered
    year = event_year[...]
    local_year = jnp.where(year < 0, -1, year & (YEAR_DEV - 1))
    hits = lax.broadcasted_iota(jnp.int32, (YEAR_DEV, year.shape[1]), 0) == local_year
    hits = jnp.where(hits, 1.0, 0.0).astype(jnp.bfloat16)
    pieces = jnp.concatenate(in_two(recovered) + in_two(retained), axis=0)
    yearly = lax.dot_general(hits, pieces, BY_ROWS, preferred_element_type=jnp.float32)
    annual = yearly[:, :count] + yearly[:, count : 2 * count]
    kept_annual = yearly[:, 2 * count : 3 * count] + yearly[:, 3 * count :]
    again = reinstatements[...].astype(jnp.float32)
    paid = jnp.minimum(annual, (1.0 + again) * limit)
    net[...] = (paid - reinstate_rate[...] * jnp.minimum(paid, again * limit)) / limit
    kept[...] = kept_annual
    half = YEAR_DEV // 2
    line = jnp.concatenate((kept_annual[:half], kept_annual[half:]), axis=1)
    for peer in range(sent.shape[0]):
        sent[peer] = line


def annual_tables(
    blocks, event_year, attach_tier, limit_tier, reinstatements, reinstate_rate, peers
):
    count = attach_tier.shape[0]
    table = jax.ShapeDtypeStruct((YEAR_DEV, count), jnp.float32)
    return pl.pallas_call(
        annual_kernel,
        out_shape=(
            table,
            table,
            jax.ShapeDtypeStruct((peers, YEAR_DEV // 2, 2 * count), jnp.float32),
        ),
        in_specs=[VMEM] * 6,
        out_specs=(VMEM, VMEM, VMEM),
        compiler_params=PARAMS,
        name="annual_tables",
    )(
        blocks,
        event_year.reshape(1, -1),
        attach_tier.reshape(1, -1),
        limit_tier.reshape(1, -1),
        reinstatements.reshape(1, -1),
        reinstate_rate.reshape(1, -1),
    )


def exchange(items, low, high):
    items[low], items[high] = (
        jnp.maximum(items[low], items[high]),
        jnp.minimum(items[low], items[high]),
    )


def sort_falling(items):
    count = len(items)
    step = 1
    while step < count:
        gap = step
        while gap >= 1:
            for base in range(gap % step, count - gap, 2 * gap):
                for at in range(base, base + min(gap, count - base - gap)):
                    if at // (2 * step) == (at + gap) // (2 * step):
                        exchange(items, at, at + gap)
            gap //= 2
        step *= 2


def larger_half(first, second):
    return [jnp.maximum(one, two) for one, two in zip(first, reversed(second))]


def sort_bitonic(items):
    gap = len(items) // 2
    while gap >= 1:
        for at in range(len(items)):
            if at & gap == 0:
                exchange(items, at, at + gap)
        gap //= 2


def outcome_kernel(everyone, kept, stop_attach, stop_width, stop_loss, tail_mean):
    peers, rows, lanes = everyone.shape
    count = lanes // 2
    tiles = [
        everyone[peer, at : at + 8, :] for peer in range(peers) for at in range(0, rows, 8)
    ]
    total = tiles[0]
    for tile in tiles[1:]:
        total = total + tile
    summed = jnp.sum(total, axis=0, keepdims=True)
    summed = summed + pltpu.roll(summed, count, 1)
    base_loss = UNIT_LOSS + summed / (peers * YEAR_DEV)
    largest = None
    for at in range(0, len(tiles), TAIL):
        group = tiles[at : at + TAIL]
        sort_falling(group)
        if largest is None:
            largest = group
        else:
            largest = larger_half(largest, group)
            sort_bitonic(largest)
    for shift in (4, 2, 1):
        largest = larger_half(largest, [pltpu.roll(item, shift, 0) for item in largest])
        sort_bitonic(largest)
    largest = larger_half(largest, [pltpu.roll(item, count, 1) for item in largest])
    top = largest[0]
    for item in largest[1:]:
        top = top + item
    tail_mean[...] = (top[0:1, :] / base_loss / TAIL)[:, :count]
    stop_loss[...] = clamp_between(
        kept[...] / base_loss[:, :count] - stop_attach[...], 0.0, stop_width[...]
    )


def outcomes(everyone, kept, stop_attach, stop_width):
    count = stop_attach.shape[0]
    return pl.pallas_call(
        outcome_kernel,
        out_shape=(
            jax.ShapeDtypeStruct(kept.shape, jnp.float32),
            jax.ShapeDtypeStruct((1, count), jnp.float32),
        ),
        in_specs=[VMEM] * 4,
        out_specs=(VMEM, VMEM),
        compiler_params=PARAMS,
        name="outcomes",
    )(everyone, kept, stop_attach.reshape(1, -1), stop_width.reshape(1, -1))


def on_device(
    event_loss,
    event_year,
    retention,
    risk_limit,
    cession_share,
    member_treaty,
    attach_tier,
    limit_tier,
    reinstatements,
    reinstate_rate,
    stop_attach,
    stop_width,
):
    ports = lax.axis_size("port")
    sums = shard_sums(event_loss, retention, risk_limit, cession_share, member_treaty)
    blocks = lax.all_to_all(
        sums.reshape(ports, -1, sums.shape[1]), "port", 0, 0, tiled=True
    )
    net, kept, sent = annual_tables(
        blocks,
        event_year,
        attach_tier,
        limit_tier,
        reinstatements,
        reinstate_rate,
        lax.axis_size("year"),
    )
    everyone = lax.all_to_all(sent, "year", 0, 0, tiled=True)
    stop_loss, tail_mean = outcomes(everyone, kept, stop_attach, stop_width)
    return (net.T, stop_loss.T, tail_mean.reshape(-1))


def solution(mesh):
    return jax.shard_map(
        on_device,
        mesh=mesh,
        in_specs=(
            P("year", "port"),
            P("year"),
            P("port"),
            P("port"),
            P("port", None),
            P("port", None),
            P("port"),
            P("port"),
            P("port"),
            P("port"),
            P("port"),
            P("port"),
        ),
        out_specs=(P("port", "year"), P("port", "year"), P("port")),
        check_vma=False,
    )
```

time: 93.9 us -> 74 us (0.79)
  blocking collectives: 0 us -> 63.4 us
  waiting for transfers between devices: 38.4 us -> 0 us
  starting transfers between devices: 25.7 us -> 0 us
  other arithmetic: 19.5 us -> 0 us
  matrix products: 5.73 us -> 0 us
  Pallas kernels: 0 us -> 4.12 us
  local copies, waits for them, and re-layouts: 3.25 us -> 5.37 us
    all_to_all x0 -> x2, blocking collectives: none -> 63.4 us  [the longest x1 38.6 us: on_device(): lax.all_to_all(sums.reshape(ports, -1, sums.shape[1]), 'port', 0, 0, tile...]
    all_to_all x2 -> x0, waiting for transfers between devices: 38.4 us -> none  [the longest x1 25.3 us: sum_at_owner(): blocks = lax.all_to_all(in_blocks(x, dim, count), axis, 0, 0, tiled=True)]
    all_to_all x2 -> x0, starting transfers between devices: 25.7 us -> none  [the longest x1 13.7 us: from_everyone(): lax.all_to_all(jnp.broadcast_to(x[None], (count, *x.shape)), axis, 0, 0,...]
    sort x6 -> x0, other arithmetic: 16.7 us -> none  [top_years(): return jnp.sort(values, axis=1)[:, values.shape[1] - keep_count:]]
    dot_general x2 -> x0, matrix products: 5.73 us -> none  [the longest x1 5.45 us: on_device(): lax.dot_general(weights, ceded_loss, contract, preferred_element_type=jnp...]
    unnamed x14 -> x24, local copies, waits for them, and re-layouts: 0.04 us -> 5.37 us
    pallas_call x0 -> x3, Pallas kernels: none -> 4.12 us  [the longest x1 2.22 us: shard_sums(): pl.pallas_call(shard_sums_kernel, out_shape=jax.ShapeDtypeStruct((TREATIE...]
    slice x20 -> x0, local copies, waits for them, and re-layouts: 2.28 us -> none  [the longest x13 1.06 us: combined_pairwise(): part[side::2]]
  transfers between devices with their start and end apart: 2 -> 0, of which waited for: 2 -> 0; matrix products, arithmetic and copies ran while one was open for 0% -> 0% of each run, Pallas kernels for 0% -> 0%
where the time goes in v1:
time: 74 us; the launch traced here: 73.6 us
  blocking collectives  63.4 us (86%)
  local copies, waits for them, and re-layouts  5.37 us (7%)
  Pallas kernels  4.12 us (6%)
    all_to_all x1, blocking collectives, on_device(): lax.all_to_all(sums.reshape(ports, -1, sums.shape[1]), 'port', 0, 0, tile...  38.6 us
    all_to_all x1, blocking collectives, on_device(): everyone = lax.all_to_all(sent, 'year', 0, 0, tiled=True)  24.9 us
    unnamed x24, local copies, waits for them, and re-layouts  5.37 us
    pallas_call x1, Pallas kernels, shard_sums(): pl.pallas_call(shard_sums_kernel, out_shape=jax.ShapeDtypeStruct((TREATIE...  2.22 us

profile of v1, /device:TPU:1, one launch (start us, length us, event | category | flops | bytes accessed | tf_op | source)
XLA Modules:
  0.0 73.6 jit_solution(11742146155258346742)
XLA Ops:
  0.6 0.0 copy-start.3
  0.6 0.7 copy-done.3
  1.3 0.0 copy-start
  1.3 1.2 %copy-done = bf16[512,1024]{1,0:T(8,128)(2,1)S(1)} copy-done((bf16[512,1024]{1,0:T(8,128)(2,1)S(1)}, bf16[512,1024]{1,0:T(8,128)(2,1)}, u32[]{:S(2)}) %copy-start) | copy-done | bytes 1048600
  2.5 0.0 copy-start.1
  2.5 0.7 copy-done.1
  3.3 0.0 copy-start.2
  3.3 0.7 copy-done.2
  4.0 0.0 copy-start.4
  4.0 0.7 copy-done.4
  4.6 2.2 %shard_sums.1 = bf16[1024,512]{1,0:T(8,128)(2,1)S(1)} custom-call(bf16[512,1024]{1,0:T(8,128)(2,1)S(1)} %copy-done, f32[1,1024]{1,0:T(1,128)S(1)} %bitcast.18, f32[1,1024]{1,0:T(1,128)S(1)} %bitcast.19, bf16[4,1024]{1,0:T(4,128)(2,1)S(1)} %bitcast.17, s32[4,1024]{1,0:T(4,128)S(1)} %bitcast.16), custom_call_target="tpu_custom_call" | custom-call | tf_op jit(solution)/shard_map/shard_sums/pallas_call | solution.py:63
  6.9 0.0 copy-start.9
  6.9 38.6 %all_to_all.10.blocks = bf16[16,64,512]{2,1,0:T(8,128)(2,1)S(1)} all-to-all(bf16[16,64,512]{2,1,0:T(8,128)(2,1)S(1)} %bitcast.15), channel_id=1, replica_groups=mesh['year'=32,'port'=16] {'port'}, dimensions={0} | all-to-all | bytes 2097152 | tf_op jit(solution)/shard_map/all_to_all | solution.py:252
  45.5 0.0 copy-start.5
  45.5 0.0 copy-done.9
  45.5 0.7 copy-done.5
  46.2 0.0 copy-done.6
  46.2 0.0 copy-done.7
  46.2 0.0 copy-done.8
  46.2 1.0 %annual_tables.1 = (f32[32,64]{1,0:T(8,128)}, f32[32,64]{1,0:T(8,128)S(1)}, f32[32,16,128]{2,1,0:T(8,128)S(1)}) custom-call(bf16[16,64,512]{2,1,0:T(8,128)(2,1)S(1)} %all_to_all.10.blocks, s32[1,512]{1,0:T(1,128)S(1)} %bitcast.20, s32[1,64]{1,0:T(1,128)S(1)} %bitcast.21, s32[1,64]{1,0:T(1,128)S(1)} %bitcast.22, s32[1,64]{1,0:T(1,128)S(1)} %bitcast.23, ...), custom_call_target="tpu_custom_call" | custom-call | tf_op jit(solution)/shard_map/annual_tables/pallas_call | solution.py:132
  47.2 24.9 %all_to_all.11.everyone = f32[32,16,128]{2,1,0:T(8,128)S(1)} all-to-all(f32[32,16,128]{2,1,0:T(8,128)S(1)} %get-tuple-element.9), channel_id=1, replica_groups=mesh['year'=32,'port'=16] {'year'}, dimensions={0} | all-to-all | bytes 524288 | tf_op jit(solution)/shard_map/all_to_all | solution.py:264
  72.1 0.7 copy-done.10
  72.7 0.0 copy-done.11
  72.7 0.9 %outcomes.1 = (f32[32,64]{1,0:T(8,128)}, f32[1,64]{1,0:T(1,128)}) custom-call(f32[32,16,128]{2,1,0:T(8,128)S(1)} %all_to_all.11.everyone, f32[32,64]{1,0:T(8,128)S(1)} %get-tuple-element.10.kept, f32[1,64]{1,0:T(1,128)S(1)} %bitcast.25, f32[1,64]{1,0:T(1,128)S(1)} %bitcast.26), custom_call_target="tpu_custom_call" | custom-call | tf_op jit(solution)/shard_map/outcomes/pallas_call | solution.py:223
  (5 shorter events, 0.0 us)
Async XLA Ops:
  0.6 0.7 copy-start.3
  1.3 1.2 %copy-start = (bf16[512,1024]{1,0:T(8,128)(2,1)S(1)}, bf16[512,1024]{1,0:T(8,128)(2,1)}, u32[]{:S(2)}) copy-start(bf16[512,1024]{1,0:T(8,128)(2,1)} %loss_hbm.1) | copy-start | bytes 3145732
  2.5 0.7 copy-start.1
  3.3 0.7 copy-start.2
  4.0 0.7 copy-start.4
  6.9 38.6 %copy-start.9 = (f32[64]{0:T(128)S(1)}, f32[64]{0:T(128)}, u32[]{:S(2)}) copy-start(f32[64]{0:T(128)} %param.21) | copy-start | bytes 772
  45.5 0.7 copy-start.5
  45.5 0.7 copy-start.6
  45.5 0.7 copy-start.7
  45.5 0.7 copy-start.8
  72.1 0.7 copy-start.10
  72.1 0.7 copy-start.11

commit v2 on v1

v2 whole, which is shorter than its diff:
```python
import jax
import jax.numpy as jnp
from jax import lax
from jax.experimental import pallas as pl
from jax.experimental.pallas import tpu as pltpu
from jax.sharding import PartitionSpec as P

TREATIES = 1024
MEMB = 4
YEAR_DEV = 32
TAIL = 16
LANES = 128
BLOCK = 256

UNIT_LOSS = 1.0

VMEM = pl.BlockSpec(memory_space=pltpu.VMEM)
HBM = pl.BlockSpec(memory_space=pltpu.HBM)
PARAMS = pltpu.CompilerParams(vmem_limit_bytes=16 * 1024 * 1024)
BY_ROWS = (((1,), (1,)), ((), ()))


def clamp_between(values, lower, upper):
    return jnp.minimum(jnp.maximum(values, lower), upper)


def shard_sums_kernel(*refs):
    inputs, (sums, table, hits), held = refs[:12], refs[12:15], refs[15:27]
    weights, ceded, arrived = refs[27:]
    order = (5, 4, 2, 3, 0, 1, 6, 7, 8, 9, 10, 11)
    fetches = {
        k: pltpu.make_async_copy(inputs[k], held[k], arrived.at[k]) for k in order
    }
    for k in order:
        fetches[k].start()
    loss, year, retention, risk_limit, share, member = held[:6]
    columns = loss.shape[1]
    treaty = lax.broadcasted_iota(jnp.int32, (BLOCK, LANES), 0)
    treaty = treaty.astype(jnp.float32).astype(jnp.bfloat16)
    zero = jnp.zeros((BLOCK, LANES), jnp.bfloat16)
    fetches[5].wait()
    fetches[4].wait()
    named = member[...]
    part = share[...]
    for first in range(0, TREATIES, BLOCK):
        local = named - first
        inside = (local >= 0) & (local < BLOCK)
        local = jnp.where(inside, local, BLOCK).astype(jnp.float32).astype(jnp.bfloat16)
        for at in range(0, columns, LANES):
            block = zero
            for slot in range(MEMB):
                hit = treaty == local[slot : slot + 1, at : at + LANES]
                block = jnp.where(hit, part[slot : slot + 1, at : at + LANES], block)
            weights[first : first + BLOCK, at : at + LANES] = block
    fetches[2].wait()
    fetches[3].wait()
    fetches[0].wait()
    ceded[...] = clamp_between(
        loss[...].astype(jnp.float32) - retention[...], 0.0, risk_limit[...]
    ).astype(jnp.bfloat16)
    for first in range(0, TREATIES, BLOCK):
        sums[first : first + BLOCK, :] = lax.dot_general(
            weights[first : first + BLOCK, :],
            ceded[...],
            BY_ROWS,
            preferred_element_type=jnp.float32,
        ).astype(jnp.bfloat16)
    fetches[1].wait()
    local_year = jnp.where(year[...] < 0, -1, year[...] & (YEAR_DEV - 1))
    hit = lax.broadcasted_iota(jnp.int32, hits.shape, 0) == local_year
    hits[...] = jnp.where(hit, 1.0, 0.0).astype(jnp.bfloat16)
    for row in range(6):
        fetches[6 + row].wait()
        table[row : row + 1, :] = held[6 + row][...].astype(jnp.float32)


def shard_sums(inputs):
    rows, columns = inputs[0].shape
    count = inputs[6].shape[0]
    views = [
        inputs[0],
        inputs[1].reshape(1, -1),
        inputs[2].reshape(1, -1),
        inputs[3].reshape(1, -1),
        inputs[4].T,
        inputs[5].T,
        *(column.reshape(1, -1) for column in inputs[6:]),
    ]
    views = [pltpu.with_memory_space_constraint(view, pltpu.HBM) for view in views]
    return pl.pallas_call(
        shard_sums_kernel,
        out_shape=(
            jax.ShapeDtypeStruct((TREATIES, rows), jnp.bfloat16),
            jax.ShapeDtypeStruct((8, count), jnp.float32),
            jax.ShapeDtypeStruct((YEAR_DEV, rows), jnp.bfloat16),
        ),
        in_specs=[HBM] * len(views),
        out_specs=(VMEM, VMEM, VMEM),
        scratch_shapes=[
            *(pltpu.VMEM(view.shape, view.dtype) for view in views),
            pltpu.VMEM((TREATIES, columns), jnp.bfloat16),
            pltpu.VMEM((rows, columns), jnp.bfloat16),
            pltpu.SemaphoreType.DMA((len(views),)),
        ],
        compiler_params=PARAMS,
        name="shard_sums",
    )(*views)


def as_column(row):
    count = row.shape[1]
    down = lax.broadcasted_iota(jnp.int32, (count, count), 0)
    across = lax.broadcasted_iota(jnp.int32, (count, count), 1)
    return jnp.sum(jnp.where(down == across, row, 0.0), axis=1, keepdims=True)


def in_two(values):
    high = values.astype(jnp.bfloat16)
    low = (values - high.astype(jnp.float32)).astype(jnp.bfloat16)
    return [high, low]


def annual_kernel(blocks, table, hits, net, kept, sent):
    count = table.shape[1]
    total = blocks[0].astype(jnp.float32)
    for shard in range(1, blocks.shape[0]):
        total = total + blocks[shard].astype(jnp.float32)
    attach = table[0:1, :] * UNIT_LOSS
    limit = table[1:2, :] * UNIT_LOSS
    again = table[2:3, :]
    rate = table[3:4, :]
    recovered = clamp_between(total - as_column(attach), 0.0, as_column(limit))
    retained = total - recovered
    pieces = jnp.concatenate(in_two(recovered) + in_two(retained), axis=0)
    yearly = lax.dot_general(hits[...], pieces, BY_ROWS, preferred_element_type=jnp.float32)
    annual = yearly[:, :count] + yearly[:, count : 2 * count]
    kept_annual = yearly[:, 2 * count : 3 * count] + yearly[:, 3 * count :]
    paid = jnp.minimum(annual, (1.0 + again) * limit)
    net[...] = (paid - rate * jnp.minimum(paid, again * limit)) / limit
    kept[...] = kept_annual
    half = YEAR_DEV // 2
    line = jnp.concatenate((kept_annual[:half], kept_annual[half:]), axis=1)
    for peer in range(sent.shape[0]):
        sent[peer] = line


def annual_tables(blocks, table, hits, peers):
    count = table.shape[1]
    tables = jax.ShapeDtypeStruct((YEAR_DEV, count), jnp.float32)
    return pl.pallas_call(
        annual_kernel,
        out_shape=(
            tables,
            tables,
            jax.ShapeDtypeStruct((peers, YEAR_DEV // 2, 2 * count), jnp.float32),
        ),
        in_specs=[VMEM] * 3,
        out_specs=(VMEM, VMEM, VMEM),
        compiler_params=PARAMS,
        name="annual_tables",
    )(blocks, table, hits)


def exchange(items, low, high):
    items[low], items[high] = (
        jnp.maximum(items[low], items[high]),
        jnp.minimum(items[low], items[high]),
    )


def sort_falling(items):
    count = len(items)
    step = 1
    while step < count:
        gap = step
        while gap >= 1:
            for base in range(gap % step, count - gap, 2 * gap):
                for at in range(base, base + min(gap, count - base - gap)):
                    if at // (2 * step) == (at + gap) // (2 * step):
                        exchange(items, at, at + gap)
            gap //= 2
        step *= 2


def larger_half(first, second):
    return [jnp.maximum(one, two) for one, two in zip(first, reversed(second))]


def sort_bitonic(items):
    gap = len(items) // 2
    while gap >= 1:
        for at in range(len(items)):
            if at & gap == 0:
                exchange(items, at, at + gap)
        gap //= 2


def outcome_kernel(everyone, kept, table, stop_loss, tail_mean):
    peers, rows, lanes = everyone.shape
    count = lanes // 2
    tiles = [
        everyone[peer, at : at + 8, :] for peer in range(peers) for at in range(0, rows, 8)
    ]
    total = tiles[0]
    for tile in tiles[1:]:
        total = total + tile
    summed = jnp.sum(total, axis=0, keepdims=True)
    summed = summed + pltpu.roll(summed, count, 1)
    base_loss = UNIT_LOSS + summed / (peers * YEAR_DEV)
    largest = None
    for at in range(0, len(tiles), TAIL):
        group = tiles[at : at + TAIL]
        sort_falling(group)
        if largest is None:
            largest = group
        else:
            largest = larger_half(largest, group)
            sort_bitonic(largest)
    for shift in (4, 2, 1):
        largest = larger_half(largest, [pltpu.roll(item, shift, 0) for item in largest])
        sort_bitonic(largest)
    largest = larger_half(largest, [pltpu.roll(item, count, 1) for item in largest])
    top = largest[0]
    for item in largest[1:]:
        top = top + item
    tail_mean[...] = (top[0:1, :] / base_loss / TAIL)[:, :count]
    stop_loss[...] = clamp_between(
        kept[...] / base_loss[:, :count] - table[4:5, :], 0.0, table[5:6, :]
    )


def outcomes(everyone, kept, table):
    return pl.pallas_call(
        outcome_kernel,
        out_shape=(
            jax.ShapeDtypeStruct(kept.shape, jnp.float32),
            jax.ShapeDtypeStruct((1, kept.shape[1]), jnp.float32),
        ),
        in_specs=[VMEM] * 3,
        out_specs=(VMEM, VMEM),
        compiler_params=PARAMS,
        name="outcomes",
    )(everyone, kept, table)


def on_device(*inputs):
    ports = lax.axis_size("port")
    sums, table, hits = shard_sums(inputs)
    blocks = lax.all_to_all(
        sums.reshape(ports, -1, sums.shape[1]), "port", 0, 0, tiled=True
    )
    net, kept, sent = annual_tables(blocks, table, hits, lax.axis_size("year"))
    everyone = lax.all_to_all(sent, "year", 0, 0, tiled=True)
    stop_loss, tail_mean = outcomes(everyone, kept, table)
    return (net.T, stop_loss.T, tail_mean.reshape(-1))


def solution(mesh):
    return jax.shard_map(
        on_device,
        mesh=mesh,
        in_specs=(
            P("year", "port"),
            P("year"),
            P("port"),
            P("port"),
            P("port", None),
            P("port", None),
            P("port"),
            P("port"),
            P("port"),
            P("port"),
            P("port"),
            P("port"),
        ),
        out_specs=(P("port", "year"), P("port", "year"), P("port")),
        check_vma=False,
    )
```

time: 74 us -> 69.3 us (0.936)
  local copies, waits for them, and re-layouts: 5.37 us -> 0 us
  Pallas kernels: 4.12 us -> 4.96 us
    unnamed x24 -> x0, local copies, waits for them, and re-layouts: 5.37 us -> none
    pallas_call x2, Pallas kernels: 3.23 us -> 4.07 us  [the longest x1 3.06 us: shard_sums(): pl.pallas_call(shard_sums_kernel, out_shape=(jax.ShapeDtypeStruct((TREATI...]
where the time goes in v2:
time: 69.3 us; the launch traced here: 69.1 us
  blocking collectives  63.4 us (91%)
  Pallas kernels  4.96 us (7%)
    all_to_all x1, blocking collectives, on_device(): lax.all_to_all(sums.reshape(ports, -1, sums.shape[1]), 'port', 0, 0, tile...  38.6 us
    all_to_all x1, blocking collectives, on_device(): everyone = lax.all_to_all(sent, 'year', 0, 0, tiled=True)  24.9 us
    pallas_call x1, Pallas kernels, shard_sums(): pl.pallas_call(shard_sums_kernel, out_shape=(jax.ShapeDtypeStruct((TREATI...  3.06 us

profile of v2, /device:TPU:1, one launch (start us, length us, event | category | flops | bytes accessed | tf_op | source)
XLA Modules:
  0.0 69.1 jit_solution(6145079633290408785)
XLA Ops:
  0.6 3.1 %shard_sums.1 = (bf16[1024,512]{1,0:T(8,128)(2,1)S(1)}, f32[8,64]{1,0:T(8,128)S(1)}, bf16[32,512]{1,0:T(8,128)(2,1)S(1)}) custom-call(bf16[512,1024]{1,0:T(8,128)(2,1)} %refs_0_.1, s32[1,512]{1,0:T(1,128)} %bitcast.20, f32[1,1024]{1,0:T(1,128)} %bitcast.18, f32[1,1024]{1,0:T(1,128)} %bitcast.19, bf16[4,1024]{1,0:T(4,128)(2,1)} %bitcast.17, ...), custom_call_target="tpu_custom_call" | custom-call | tf_op jit(solution)/shard_map/shard_sums/pallas_call | solution.py:90
  3.7 38.6 %all_to_all.10.blocks = bf16[16,64,512]{2,1,0:T(8,128)(2,1)S(1)} all-to-all(bf16[16,64,512]{2,1,0:T(8,128)(2,1)S(1)} %bitcast.15), channel_id=1, replica_groups=mesh['year'=32,'port'=16] {'port'}, dimensions={0} | all-to-all | bytes 2097152 | tf_op jit(solution)/shard_map/all_to_all | solution.py:249
  42.3 1.0 %annual_tables.1 = (f32[32,64]{1,0:T(8,128)}, f32[32,64]{1,0:T(8,128)S(1)}, f32[32,16,128]{2,1,0:T(8,128)S(1)}) custom-call(bf16[16,64,512]{2,1,0:T(8,128)(2,1)S(1)} %all_to_all.10.blocks, f32[8,64]{1,0:T(8,128)S(1)} %get-tuple-element.12.table, bf16[32,512]{1,0:T(8,128)(2,1)S(1)} %get-tuple-element.13.hits), custom_call_target="tpu_custom_call" | custom-call | tf_op jit(solution)/shard_map/annual_tables/pallas_call | solution.py:150
  43.3 24.9 %all_to_all.11.everyone = f32[32,16,128]{2,1,0:T(8,128)S(1)} all-to-all(f32[32,16,128]{2,1,0:T(8,128)S(1)} %get-tuple-element.15), channel_id=1, replica_groups=mesh['year'=32,'port'=16] {'year'}, dimensions={0} | all-to-all | bytes 524288 | tf_op jit(solution)/shard_map/all_to_all | solution.py:253
  68.2 0.9 %outcomes.1 = (f32[32,64]{1,0:T(8,128)}, f32[1,64]{1,0:T(1,128)}) custom-call(f32[32,16,128]{2,1,0:T(8,128)S(1)} %all_to_all.11.everyone, f32[32,64]{1,0:T(8,128)S(1)} %get-tuple-element.16.kept, f32[8,64]{1,0:T(8,128)S(1)} %get-tuple-element.12.table), custom_call_target="tpu_custom_call" | custom-call | tf_op jit(solution)/shard_map/outcomes/pallas_call | solution.py:233

commit v3 on v2

--- a/solution.py
+++ b/solution.py
@@ -42,7 +42,8 @@
     fetches[4].wait()
     named = member[...]
     part = share[...]
-    for first in range(0, TREATIES, BLOCK):
+
+    def build(first):
         local = named - first
         inside = (local >= 0) & (local < BLOCK)
         local = jnp.where(inside, local, BLOCK).astype(jnp.float32).astype(jnp.bfloat16)
@@ -52,19 +53,29 @@
                 hit = treaty == local[slot : slot + 1, at : at + LANES]
                 block = jnp.where(hit, part[slot : slot + 1, at : at + LANES], block)
             weights[first : first + BLOCK, at : at + LANES] = block
+
+    def multiply(first):
+        sums[first : first + BLOCK, :] = lax.dot_general(
+            weights[first : first + BLOCK, :],
+            ceded[...],
+            BY_ROWS,
+            preferred_element_type=jnp.float32,
+        ).astype(jnp.bfloat16)
+
+    blocks = list(range(0, TREATIES, BLOCK))
+    ahead = 2
+    for first in blocks[:ahead]:
+        build(first)
     fetches[2].wait()
     fetches[3].wait()
     fetches[0].wait()
     ceded[...] = clamp_between(
         loss[...].astype(jnp.float32) - retention[...], 0.0, risk_limit[...]
     ).astype(jnp.bfloat16)
-    for first in range(0, TREATIES, BLOCK):
-        sums[first : first + BLOCK, :] = lax.dot_general(
-            weights[first : first + BLOCK, :],
-            ceded[...],
-            BY_ROWS,
-            preferred_element_type=jnp.float32,
-        ).astype(jnp.bfloat16)
+    for k, first in enumerate(blocks):
+        multiply(first)
+        if k + ahead < len(blocks):
+            build(blocks[k + ahead])
     fetches[1].wait()
     local_year = jnp.where(year[...] < 0, -1, year[...] & (YEAR_DEV - 1))
     hit = lax.broadcasted_iota(jnp.int32, hits.shape, 0) == local_year
@@ -120,23 +131,19 @@
     return [high, low]
 
 
-def annual_kernel(blocks, table, hits, net, kept, sent):
+def annual_kernel(blocks, table, hits, annual, kept, sent):
     count = table.shape[1]
     total = blocks[0].astype(jnp.float32)
     for shard in range(1, blocks.shape[0]):
         total = total + blocks[shard].astype(jnp.float32)
     attach = table[0:1, :] * UNIT_LOSS
     limit = table[1:2, :] * UNIT_LOSS
-    again = table[2:3, :]
-    rate = table[3:4, :]
     recovered = clamp_between(total - as_column(attach), 0.0, as_column(limit))
     retained = total - recovered
     pieces = jnp.concatenate(in_two(recovered) + in_two(retained), axis=0)
     yearly = lax.dot_general(hits[...], pieces, BY_ROWS, preferred_element_type=jnp.float32)
-    annual = yearly[:, :count] + yearly[:, count : 2 * count]
+    annual[...] = yearly[:, :count] + yearly[:, count : 2 * count]
     kept_annual = yearly[:, 2 * count : 3 * count] + yearly[:, 3 * count :]
-    paid = jnp.minimum(annual, (1.0 + again) * limit)
-    net[...] = (paid - rate * jnp.minimum(paid, again * limit)) / limit
     kept[...] = kept_annual
     half = YEAR_DEV // 2
     line = jnp.concatenate((kept_annual[:half], kept_annual[half:]), axis=1)
@@ -195,7 +202,12 @@
         gap //= 2
 
 
-def outcome_kernel(everyone, kept, table, stop_loss, tail_mean):
+def outcome_kernel(everyone, annual, kept, table, net, stop_loss, tail_mean):
+    limit = table[1:2, :] * UNIT_LOSS
+    again = table[2:3, :]
+    rate = table[3:4, :]
+    paid = jnp.minimum(annual[...], (1.0 + again) * limit)
+    net[...] = (paid - rate * jnp.minimum(paid, again * limit)) / limit
     peers, rows, lanes = everyone.shape
     count = lanes // 2
     tiles = [
@@ -229,18 +241,19 @@
     )
 
 
-def outcomes(everyone, kept, table):
+def outcomes(everyone, annual, kept, table):
     return pl.pallas_call(
         outcome_kernel,
         out_shape=(
             jax.ShapeDtypeStruct(kept.shape, jnp.float32),
+            jax.ShapeDtypeStruct(kept.shape, jnp.float32),
             jax.ShapeDtypeStruct((1, kept.shape[1]), jnp.float32),
         ),
-        in_specs=[VMEM] * 3,
-        out_specs=(VMEM, VMEM),
+        in_specs=[VMEM] * 4,
+        out_specs=(VMEM, VMEM, VMEM),
         compiler_params=PARAMS,
         name="outcomes",
-    )(everyone, kept, table)
+    )(everyone, annual, kept, table)
 
 
 def on_device(*inputs):
@@ -249,9 +262,9 @@
     blocks = lax.all_to_all(
         sums.reshape(ports, -1, sums.shape[1]), "port", 0, 0, tiled=True
     )
-    net, kept, sent = annual_tables(blocks, table, hits, lax.axis_size("year"))
+    annual, kept, sent = annual_tables(blocks, table, hits, lax.axis_size("year"))
     everyone = lax.all_to_all(sent, "year", 0, 0, tiled=True)
-    stop_loss, tail_mean = outcomes(everyone, kept, table)
+    net, stop_loss, tail_mean = outcomes(everyone, annual, kept, table)
     return (net.T, stop_loss.T, tail_mean.reshape(-1))
 
 

time: 69.3 us -> 68.6 us (0.990)
  Pallas kernels: 4.96 us -> 4.23 us
where the time goes in v3:
time: 68.6 us; the launch traced here: 68.3 us
  blocking collectives  63.5 us (93%)
  Pallas kernels  4.23 us (6%)
    all_to_all x1, blocking collectives, on_device(): lax.all_to_all(sums.reshape(ports, -1, sums.shape[1]), 'port', 0, 0, tile...  38.6 us
    all_to_all x1, blocking collectives, on_device(): everyone = lax.all_to_all(sent, 'year', 0, 0, tiled=True)  24.9 us
    pallas_call x1, Pallas kernels, shard_sums(): pl.pallas_call(shard_sums_kernel, out_shape=(jax.ShapeDtypeStruct((TREATI...  2.86 us

profile of v3, /device:TPU:1, one launch (start us, length us, event | category | flops | bytes accessed | tf_op | source)
XLA Modules:
  0.0 68.3 jit_solution(7425856655015198777)
XLA Ops:
  0.6 2.9 %shard_sums.1 = (bf16[1024,512]{1,0:T(8,128)(2,1)S(1)}, f32[8,64]{1,0:T(8,128)S(1)}, bf16[32,512]{1,0:T(8,128)(2,1)S(1)}) custom-call(bf16[512,1024]{1,0:T(8,128)(2,1)} %refs_0_.1, s32[1,512]{1,0:T(1,128)} %bitcast.20, f32[1,1024]{1,0:T(1,128)} %bitcast.18, f32[1,1024]{1,0:T(1,128)} %bitcast.19, bf16[4,1024]{1,0:T(4,128)(2,1)} %bitcast.17, ...), custom_call_target="tpu_custom_call" | custom-call | tf_op jit(solution)/shard_map/shard_sums/pallas_call | solution.py:101
  3.5 38.6 %all_to_all.10.blocks = bf16[16,64,512]{2,1,0:T(8,128)(2,1)S(1)} all-to-all(bf16[16,64,512]{2,1,0:T(8,128)(2,1)S(1)} %bitcast.15), channel_id=1, replica_groups=mesh['year'=32,'port'=16] {'port'}, dimensions={0} | all-to-all | bytes 2097152 | tf_op jit(solution)/shard_map/all_to_all | solution.py:262
  42.1 0.5 annual_tables.1
  42.6 24.9 %all_to_all.11.everyone = f32[32,16,128]{2,1,0:T(8,128)S(1)} all-to-all(f32[32,16,128]{2,1,0:T(8,128)S(1)} %get-tuple-element.15), channel_id=1, replica_groups=mesh['year'=32,'port'=16] {'year'}, dimensions={0} | all-to-all | bytes 524288 | tf_op jit(solution)/shard_map/all_to_all | solution.py:266
  67.5 0.9 %outcomes.1 = (f32[32,64]{1,0:T(8,128)}, f32[32,64]{1,0:T(8,128)}, f32[1,64]{1,0:T(1,128)}) custom-call(f32[32,16,128]{2,1,0:T(8,128)S(1)} %all_to_all.11.everyone, f32[32,64]{1,0:T(8,128)S(1)} %get-tuple-element.16.annual, f32[32,64]{1,0:T(8,128)S(1)} %get-tuple-element.17.kept, f32[8,64]{1,0:T(8,128)S(1)} %get-tuple-element.13.table), custom_call_target="tpu_custom_call" | custom-call | tf_op jit(solution)/shard_map/outcomes/pallas_call | solution.py:245

commit v4 on v3

--- a/solution.py
+++ b/solution.py
@@ -147,6 +147,7 @@
     kept[...] = kept_annual
     half = YEAR_DEV // 2
     line = jnp.concatenate((kept_annual[:half], kept_annual[half:]), axis=1)
+    line = line.astype(jnp.bfloat16)
     for peer in range(sent.shape[0]):
         sent[peer] = line
 
@@ -159,7 +160,7 @@
         out_shape=(
             tables,
             tables,
-            jax.ShapeDtypeStruct((peers, YEAR_DEV // 2, 2 * count), jnp.float32),
+            jax.ShapeDtypeStruct((peers, YEAR_DEV // 2, 2 * count), jnp.bfloat16),
         ),
         in_specs=[VMEM] * 3,
         out_specs=(VMEM, VMEM, VMEM),
@@ -211,7 +212,9 @@
     peers, rows, lanes = everyone.shape
     count = lanes // 2
     tiles = [
-        everyone[peer, at : at + 8, :] for peer in range(peers) for at in range(0, rows, 8)
+        line[at : at + 8, :]
+        for line in (everyone[peer].astype(jnp.float32) for peer in range(peers))
+        for at in range(0, rows, 8)
     ]
     total = tiles[0]
     for tile in tiles[1:]:

time: 68.6 us -> 66.1 us (0.964)
  blocking collectives: 63.5 us -> 60.9 us
    all_to_all x1, blocking collectives: 24.9 us -> 22.3 us  [on_device(): everyone = lax.all_to_all(sent, 'year', 0, 0, tiled=True)]
where the time goes in v4:
time: 66.1 us; the launch traced here: 65.8 us
  blocking collectives  60.9 us (92%)
  Pallas kernels  4.24 us (6%)
    all_to_all x1, blocking collectives, on_device(): lax.all_to_all(sums.reshape(ports, -1, sums.shape[1]), 'port', 0, 0, tile...  38.6 us
    all_to_all x1, blocking collectives, on_device(): everyone = lax.all_to_all(sent, 'year', 0, 0, tiled=True)  22.3 us
    pallas_call x1, Pallas kernels, shard_sums(): pl.pallas_call(shard_sums_kernel, out_shape=(jax.ShapeDtypeStruct((TREATI...  2.86 us

profile of v4, /device:TPU:1, one launch (start us, length us, event | category | flops | bytes accessed | tf_op | source)
XLA Modules:
  0.0 65.8 jit_solution(4433480754612248173)
XLA Ops:
  0.6 2.9 %shard_sums.1 = (bf16[1024,512]{1,0:T(8,128)(2,1)S(1)}, f32[8,64]{1,0:T(8,128)S(1)}, bf16[32,512]{1,0:T(8,128)(2,1)S(1)}) custom-call(bf16[512,1024]{1,0:T(8,128)(2,1)} %refs_0_.1, s32[1,512]{1,0:T(1,128)} %bitcast.20, f32[1,1024]{1,0:T(1,128)} %bitcast.18, f32[1,1024]{1,0:T(1,128)} %bitcast.19, bf16[4,1024]{1,0:T(4,128)(2,1)} %bitcast.17, ...), custom_call_target="tpu_custom_call" | custom-call | tf_op jit(solution)/shard_map/shard_sums/pallas_call | solution.py:101
  3.5 38.6 %all_to_all.10.blocks = bf16[16,64,512]{2,1,0:T(8,128)(2,1)S(1)} all-to-all(bf16[16,64,512]{2,1,0:T(8,128)(2,1)S(1)} %bitcast.15), channel_id=1, replica_groups=mesh['year'=32,'port'=16] {'port'}, dimensions={0} | all-to-all | bytes 2097152 | tf_op jit(solution)/shard_map/all_to_all | solution.py:265
  42.1 0.5 annual_tables.1
  42.6 22.3 %all_to_all.11.everyone = bf16[32,16,128]{2,1,0:T(8,128)(2,1)S(1)} all-to-all(bf16[32,16,128]{2,1,0:T(8,128)(2,1)S(1)} %get-tuple-element.15), channel_id=1, replica_groups=mesh['year'=32,'port'=16] {'year'}, dimensions={0} | all-to-all | bytes 262144 | tf_op jit(solution)/shard_map/all_to_all | solution.py:269
  64.9 0.9 %outcomes.1 = (f32[32,64]{1,0:T(8,128)}, f32[32,64]{1,0:T(8,128)}, f32[1,64]{1,0:T(1,128)}) custom-call(bf16[32,16,128]{2,1,0:T(8,128)(2,1)S(1)} %all_to_all.11.everyone, f32[32,64]{1,0:T(8,128)S(1)} %get-tuple-element.16.annual, f32[32,64]{1,0:T(8,128)S(1)} %get-tuple-element.17.kept, f32[8,64]{1,0:T(8,128)S(1)} %get-tuple-element.13.table), custom_call_target="tpu_custom_call" | custom-call | tf_op jit(solution)/shard_map/outcomes/pallas_call | solution.py:248

commit v5 on v4

--- a/solution.py
+++ b/solution.py
@@ -15,6 +15,7 @@
 UNIT_LOSS = 1.0
 
 VMEM = pl.BlockSpec(memory_space=pltpu.VMEM)
+SMEM = pl.BlockSpec(memory_space=pltpu.SMEM)
 HBM = pl.BlockSpec(memory_space=pltpu.HBM)
 PARAMS = pltpu.CompilerParams(vmem_limit_bytes=16 * 1024 * 1024)
 BY_ROWS = (((1,), (1,)), ((), ()))
@@ -25,8 +26,9 @@
 
 
 def shard_sums_kernel(*refs):
-    inputs, (sums, table, hits), held = refs[:12], refs[12:15], refs[15:27]
-    weights, ceded, arrived = refs[27:]
+    inputs, outputs, held = refs[:12], refs[12:17], refs[17:29]
+    sums, first_sums, table, hits, short = outputs
+    weights, ceded, arrived = refs[29:]
     order = (5, 4, 2, 3, 0, 1, 6, 7, 8, 9, 10, 11)
     fetches = {
         k: pltpu.make_async_copy(inputs[k], held[k], arrived.at[k]) for k in order
@@ -55,12 +57,14 @@
             weights[first : first + BLOCK, at : at + LANES] = block
 
     def multiply(first):
-        sums[first : first + BLOCK, :] = lax.dot_general(
+        block = lax.dot_general(
             weights[first : first + BLOCK, :],
             ceded[...],
             BY_ROWS,
             preferred_element_type=jnp.float32,
         ).astype(jnp.bfloat16)
+        sums[first : first + BLOCK, :] = block
+        first_sums[first : first + BLOCK, :] = block[:, : first_sums.shape[1]]
 
     blocks = list(range(0, TREATIES, BLOCK))
     ahead = 2
@@ -80,6 +84,8 @@
     local_year = jnp.where(year[...] < 0, -1, year[...] & (YEAR_DEV - 1))
     hit = lax.broadcasted_iota(jnp.int32, hits.shape, 0) == local_year
     hits[...] = jnp.where(hit, 1.0, 0.0).astype(jnp.bfloat16)
+    late = lax.broadcasted_iota(jnp.int32, year.shape, 1) >= first_sums.shape[1]
+    short[0] = 1 - jnp.max(jnp.where(late & (year[...] >= 0), 1, 0))
     for row in range(6):
         fetches[6 + row].wait()
         table[row : row + 1, :] = held[6 + row][...].astype(jnp.float32)
@@ -102,11 +108,13 @@
         shard_sums_kernel,
         out_shape=(
             jax.ShapeDtypeStruct((TREATIES, rows), jnp.bfloat16),
+            jax.ShapeDtypeStruct((TREATIES, rows // 2), jnp.bfloat16),
             jax.ShapeDtypeStruct((8, count), jnp.float32),
             jax.ShapeDtypeStruct((YEAR_DEV, rows), jnp.bfloat16),
+            jax.ShapeDtypeStruct((1,), jnp.int32),
         ),
         in_specs=[HBM] * len(views),
-        out_specs=(VMEM, VMEM, VMEM),
+        out_specs=(VMEM, VMEM, VMEM, VMEM, SMEM),
         scratch_shapes=[
             *(pltpu.VMEM(view.shape, view.dtype) for view in views),
             pltpu.VMEM((TREATIES, columns), jnp.bfloat16),
@@ -141,7 +149,9 @@
     recovered = clamp_between(total - as_column(attach), 0.0, as_column(limit))
     retained = total - recovered
     pieces = jnp.concatenate(in_two(recovered) + in_two(retained), axis=0)
-    yearly = lax.dot_general(hits[...], pieces, BY_ROWS, preferred_element_type=jnp.float32)
+    yearly = lax.dot_general(
+        hits[:, : total.shape[1]], pieces, BY_ROWS, preferred_element_type=jnp.float32
+    )
     annual[...] = yearly[:, :count] + yearly[:, count : 2 * count]
     kept_annual = yearly[:, 2 * count : 3 * count] + yearly[:, 3 * count :]
     kept[...] = kept_annual
@@ -261,11 +271,18 @@
 
 def on_device(*inputs):
     ports = lax.axis_size("port")
-    sums, table, hits = shard_sums(inputs)
-    blocks = lax.all_to_all(
-        sums.reshape(ports, -1, sums.shape[1]), "port", 0, 0, tiled=True
-    )
-    annual, kept, sent = annual_tables(blocks, table, hits, lax.axis_size("year"))
+    years = lax.axis_size("year")
+    sums, first_sums, table, hits, short = shard_sums(inputs)
+
+    def exchanged(rows):
+        blocks = lax.all_to_all(
+            rows.reshape(ports, -1, rows.shape[1]), "port", 0, 0, tiled=True
+        )
+        return annual_tables(blocks, table, hits, years)
+
+    annual, kept, sent = lax.cond(
+        short[0] == 1, lambda: exchanged(first_sums), lambda: exchanged(sums)
+    )
     everyone = lax.all_to_all(sent, "year", 0, 0, tiled=True)
     net, stop_loss, tail_mean = outcomes(everyone, annual, kept, table)
     return (net.T, stop_loss.T, tail_mean.reshape(-1))

time: 66.1 us -> 62.6 us (0.947)
  blocking collectives: 60.9 us -> 56.6 us
    all_to_all x1, blocking collectives: 38.6 us -> 27.4 us  [exchanged(): lax.all_to_all(rows.reshape(ports, -1, rows.shape[1]), 'port', 0, 0, tile...]
    all_to_all x1, blocking collectives: 22.3 us -> 29.2 us  [on_device(): everyone = lax.all_to_all(sent, 'year', 0, 0, tiled=True)]
    pallas_call x1, Pallas kernels: 2.86 us -> 3.58 us  [shard_sums(): pl.pallas_call(shard_sums_kernel, out_shape=(jax.ShapeDtypeStruct((TREATI...]
where the time goes in v5:
time: 62.6 us; the launch traced here: 62.8 us
  blocking collectives  56.6 us (90%)
  Pallas kernels  4.89 us (8%)
  between operations  1.3 us (2%)
    all_to_all x1, blocking collectives, on_device(): everyone = lax.all_to_all(sent, 'year', 0, 0, tiled=True)  29.2 us
    all_to_all x1, blocking collectives, exchanged(): lax.all_to_all(rows.reshape(ports, -1, rows.shape[1]), 'port', 0, 0, tile...  27.4 us
    pallas_call x1, Pallas kernels, shard_sums(): pl.pallas_call(shard_sums_kernel, out_shape=(jax.ShapeDtypeStruct((TREATI...  3.58 us

profile of v5, /device:TPU:1, one launch (start us, length us, event | category | flops | bytes accessed | tf_op | source)
XLA Modules:
  0.0 62.8 jit_solution(451350659365904456)
XLA Ops:
  0.6 3.6 %shard_sums.1 = (bf16[1024,512]{1,0:T(8,128)(2,1)S(1)}, bf16[1024,256]{1,0:T(8,128)(2,1)S(1)}, f32[8,64]{1,0:T(8,128)S(1)}, bf16[32,512]{1,0:T(8,128)(2,1)S(1)}, s32[1]{0:T(128)}) custom-call(bf16[512,1024]{1,0:T(8,128)(2,1)} %refs_0_.1, s32[1,512]{1,0:T(1,128)} %bitcast.23, f32[1,1024]{1,0:T(1,128)} %bitcast.21, f32[1,1024]{1,0:T(1,128)} %bitcast.22, ...), custom_call_target="tpu_custom_call" | custom-call | tf_op jit(solution)/shard_map/shard_sums/pallas_call | solution.py:107
  4.9 27.8 %conditional.1 = ((f32[32,64]{1,0:T(8,128)S(1)}, f32[32,64]{1,0:T(8,128)S(1)}, bf16[32,16,128]{2,1,0:T(8,128)(2,1)S(1)})) conditional(s32[]{:T(128)} %bitcast.13, (bf16[1024,512]{1,0:T(8,128)(2,1)S(1)}, f32[8,64]{1,0:T(8,128)S(1)}, bf16[32,512]{1,0:T(8,128)(2,1)S(1)}) %tuple.14, (bf16[1024,256]{1,0:T(8,128)(2,1)S(1)}, f32[8,64]{1,0:T(8,128)S(1)}, ...), branch_computations={%region_0.0_spmd, %region_1.0_spmd} | conditional | bytes 2097160 | solution.py:283
  4.9 27.4 %all_to_all.14.blocks = bf16[16,64,256]{2,1,0:T(8,128)(2,1)S(1)} all-to-all(bf16[16,64,256]{2,1,0:T(8,128)(2,1)S(1)} %bitcast.18), channel_id=1, replica_groups=mesh['year'=32,'port'=16] {'port'}, dimensions={0} | all-to-all | bytes 1048576 | tf_op jit(solution)/shard_map/cond/branch_1_fun/all_to_all | solution.py:278
  32.3 0.4 annual_tables.3
  32.7 29.2 %all_to_all.15.everyone = bf16[32,16,128]{2,1,0:T(8,128)(2,1)S(1)} all-to-all(bf16[32,16,128]{2,1,0:T(8,128)(2,1)S(1)} %get-tuple-element.37), channel_id=1, replica_groups=mesh['year'=32,'port'=16] {'year'}, dimensions={0} | all-to-all | bytes 262144 | tf_op jit(solution)/shard_map/all_to_all | solution.py:286
  61.9 0.9 %outcomes.1 = (f32[32,64]{1,0:T(8,128)}, f32[32,64]{1,0:T(8,128)}, f32[1,64]{1,0:T(1,128)}) custom-call(bf16[32,16,128]{2,1,0:T(8,128)(2,1)S(1)} %all_to_all.15.everyone, f32[32,64]{1,0:T(8,128)S(1)} %get-tuple-element.38.annual, f32[32,64]{1,0:T(8,128)S(1)} %get-tuple-element.39.kept, f32[8,64]{1,0:T(8,128)S(1)} %get-tuple-element.34.table), custom_call_target="tpu_custom_call" | custom-call | tf_op jit(solution)/shard_map/outcomes/pallas_call | solution.py:258
